TPU v7x, 512 devices: a whole 4x4x16 slice. The times are simulated.
512 devices in a mesh: ref: 16 (over x, y_lo, core), dom: 32 (over z, y_hi).
Axes of the slice: x: 4, y: 4 (y_hi: 2, y_lo: 2; y = y_hi * 2 + y_lo), z: 16, core: 2. Of those that a mesh axis runs over, the one named last changes fastest.
Arguments:
- particles: bfloat16 [8192, 7168], P(('ref', 'dom')), may hold values from -16 to 16
- offsets: int32 [8192], P(('ref', 'dom')), may hold values from 0 to 8, as said below
- references: bfloat16 [512, 7168], P('ref'), may hold values from -0.6 to 0.6
- noise_weight: float32 [3584], replicated, may hold values from 0.06 to 0.24
- ref_class: int32 [512], replicated, may hold values from 0 to 7
- ref_orient: int32 [512], replicated, may hold values from 0 to 63
- class_logprior: float32 [8], replicated, may hold values from -1 to 1
- orient_logprior: float32 [64], replicated, may hold values from -1 to 1
Outputs:
- log_post: float32 [8192, 9, 512], P(('ref', 'dom'))
- class_sums: float32 [8, 7168], P(None, ('ref', 'dom'))
Inputs may be any that keep to these rules, and one draw needn't show every extreme that they name: `offsets`: index of the prior's centre: horizontal step (o mod 3) - 1 pixels, vertical step floor(o / 3) - 1 pixels.
All inputs are finite; a program needn't handle non-finite values.
Results may differ from a plain program's by a relative error of at most 0.0042.
Values may be sent and summed in bfloat16 or wider, within the bound.
A program may use at most 64 MiB of HBM per device.

v0:
```python
import math
import jax
import jax.numpy as jnp
from jax import lax
from jax.sharding import PartitionSpec as P

SHIFTS = 9


def in_blocks(shard, dim, length):
    before, after = (shard.shape[:dim], shard.shape[dim + 1 :])
    return jnp.moveaxis(shard.reshape(*before, length, -1, *after), dim, 0)


def sum_at_owner(shard, axis, dim):
    length = lax.axis_size(axis)
    blocks = lax.all_to_all(in_blocks(shard, dim, length), axis, 0, 0, tiled=True)
    return jnp.sum(blocks, axis=0)


def shift_tables(count):
    coeffs = jnp.arange(count, dtype=jnp.int32)
    column_freq = (coeffs % 56).astype(jnp.float32)
    row_freq = (coeffs // 56 - 32).astype(jnp.float32)
    shift_ids = jnp.arange(SHIFTS, dtype=jnp.int32)
    step_right = (shift_ids % 3 - 1).astype(jnp.float32)
    step_down = (shift_ids // 3 - 1).astype(jnp.float32)
    turning = (
        2.0
        * math.pi
        / 96.0
        * (step_right[:, None] * column_freq[None, :] + step_down[:, None] * row_freq[None, :])
    )
    return (jnp.cos(turning), jnp.sin(turning))


def centre_prior(offsets):
    shift_ids = jnp.arange(SHIFTS, dtype=jnp.int32)
    step_right = (shift_ids % 3 - 1).astype(jnp.float32)
    step_down = (shift_ids // 3 - 1).astype(jnp.float32)
    centre_right = (offsets % 3 - 1).astype(jnp.float32)
    centre_down = (offsets // 3 - 1).astype(jnp.float32)
    apart_right = step_right[None, :] - centre_right[:, None]
    apart_down = step_down[None, :] - centre_down[:, None]
    return -0.5 * (apart_right * apart_right + apart_down * apart_down)


def aligned_stack(real_part, imag_part, cosine_table, sine_table, twice):
    turned_real = (
        real_part[:, None, :] * cosine_table[None] - imag_part[:, None, :] * sine_table[None]
    )
    turned_imag = (
        real_part[:, None, :] * sine_table[None] + imag_part[:, None, :] * cosine_table[None]
    )
    stacked_rows = real_part.shape[0] * cosine_table.shape[0]
    scaled_real = (
        (turned_real * twice[None, None, :])
        .astype(jnp.bfloat16)
        .reshape(stacked_rows, real_part.shape[1])
    )
    scaled_imag = (
        (turned_imag * twice[None, None, :])
        .astype(jnp.bfloat16)
        .reshape(stacked_rows, real_part.shape[1])
    )
    return (scaled_real, scaled_imag)


def contract(left, right):
    return lax.dot_general(
        left, right, (((1,), (1,)), ((), ())), preferred_element_type=jnp.float32
    )


def local(
    particles,
    offsets,
    references,
    noise_weight,
    ref_class,
    ref_orient,
    class_logprior,
    orient_logprior,
):
    local_rows = particles.shape[0]
    coef_total = particles.shape[1] // 2
    ref_total = ref_class.shape[0]
    class_count = class_logprior.shape[0]
    cosine_table, sine_table = shift_tables(coef_total)
    twice = 2.0 * noise_weight
    values = particles.astype(jnp.float32)
    real_part = values[:, :coef_total]
    imag_part = values[:, coef_total:]
    scaled_real, scaled_imag = aligned_stack(real_part, imag_part, cosine_table, sine_table, twice)
    class_table = (ref_class[:, None] == jnp.arange(class_count, dtype=jnp.int32)[None, :]).astype(
        jnp.float32
    )
    orient_table = (
        ref_orient[:, None] == jnp.arange(orient_logprior.shape[0], dtype=jnp.int32)[None, :]
    ).astype(jnp.float32)
    prior = jnp.dot(class_table, class_logprior, precision=lax.Precision.HIGHEST) + jnp.dot(
        orient_table, orient_logprior, precision=lax.Precision.HIGHEST
    )
    segment = lax.all_gather(references, "ref", axis=0, tiled=True)
    cross_piece = contract(scaled_real, segment[:, :coef_total]) + contract(
        scaled_imag, segment[:, coef_total:]
    )
    wide = segment.astype(jnp.float32)
    norm_piece = jnp.sum(
        noise_weight[None, :]
        * (
            wide[:, :coef_total] * wide[:, :coef_total]
            + wide[:, coef_total:] * wide[:, coef_total:]
        ),
        axis=1,
    )
    scores = (
        cross_piece.reshape(local_rows, SHIFTS, ref_total)
        - norm_piece[None, None, :]
        + prior[None, None, :]
        + centre_prior(offsets)[:, :, None]
    )
    row_peak = jnp.max(scores, axis=(1, 2), keepdims=True)
    log_total = row_peak + jnp.log(jnp.sum(jnp.exp(scores - row_peak), axis=(1, 2), keepdims=True))
    log_post = scores - log_total
    class_post = jnp.dot(
        jnp.exp(log_post).reshape(local_rows * SHIFTS, ref_total),
        class_table,
        precision=lax.Precision.HIGHEST,
    ).reshape(local_rows, SHIFTS, class_count)
    sums_real = jnp.einsum("ntc,nk->tck", class_post, real_part, precision=lax.Precision.HIGHEST)
    sums_imag = jnp.einsum("ntc,nk->tck", class_post, imag_part, precision=lax.Precision.HIGHEST)
    class_real = jnp.einsum(
        "tk,tck->ck", cosine_table, sums_real, precision=lax.Precision.HIGHEST
    ) - jnp.einsum("tk,tck->ck", sine_table, sums_imag, precision=lax.Precision.HIGHEST)
    class_imag = jnp.einsum(
        "tk,tck->ck", sine_table, sums_real, precision=lax.Precision.HIGHEST
    ) + jnp.einsum("tk,tck->ck", cosine_table, sums_imag, precision=lax.Precision.HIGHEST)
    devices = lax.axis_size(("ref", "dom"))
    partial_value = jnp.concatenate([class_real, class_imag], axis=1) * (
        1.0 / math.sqrt(local_rows * devices)
    )
    by_ref = sum_at_owner(partial_value, "ref", 1)
    class_sums = sum_at_owner(by_ref, "dom", 1)
    return (log_post, class_sums)


def solution(mesh):
    return jax.shard_map(
        local,
        mesh=mesh,
        in_specs=(
            P(("ref", "dom"), None),
            P(("ref", "dom")),
            P("ref", None),
            P(),
            P(),
            P(),
            P(),
            P(),
        ),
        out_specs=(P(("ref", "dom"), None, None), P(None, ("ref", "dom"))),
        check_vma=False,
    )
```

profile of v0, /device:TPU:32, one launch (start us, length us, event | category | flops | bytes accessed | tf_op | source)
XLA Modules:
  0.0 147.3 jit_solution(8516085216977881511)
XLA Ops:
  7.2 0.7 all-gather.2.cloned.1.call-update
  7.9 0.1 sub.250
  8.0 0.7 fusion.43
  8.7 0.1 sub.241
  8.8 0.1 sub.251
  8.9 0.1 sub.246
  9.0 0.1 sub.236
  9.0 0.1 sub.247
  9.2 1.0 fusion.46
  10.1 1.6 %fusion.23 = (f32[3584,9]{0,1:T(8,128)S(1)}, f32[3584,9]{0,1:T(8,128)}, f32[9,3584]{1,0:T(8,128)S(1)}, f32[9,3584]{1,0:T(8,128)S(1)}) fusion(f32[3584]{0:T(1024)S(1)} %get-tuple-element.26, f32[9]{0:T(128)S(1)} %get-tuple-element.29, f32[3584]{0:T(1024)S(1)} %get-tuple-element.27, f32[9]{0:T(128)S(1)} %get-tuple-element.28), kind=kLoop, calls=%fused_computation.43 | loop fusion | flops 129024 | bytes 544840
  11.7 4.0 %multiply_subtract_fusion = (f32[16,9,3584]{2,1,0:T(8,128)}, f32[16,9,3584]{2,1,0:T(8,128)}) fusion(f32[9,3584]{1,0:T(8,128)S(1)} %get-tuple-element.20, f32[16,3584]{1,0:T(8,128)S(1)} %get-tuple-element.17, f32[9,3584]{1,0:T(8,128)S(1)} %get-tuple-element.21, f32[16,3584]{1,0:T(8,128)S(1)} %get-tuple-element.16), kind=kLoop, calls=%fused_computation.12 | loop fusion | flops 3096576 | bytes 4845568 | tf_op jit(solution)/shard_map/sub | solution.py:50
  15.7 3.2 %add.202 = f32[144,3584]{1,0:T(8,128)} reshape(f32[16,9,3584]{2,1,0:T(8,128)} %get-tuple-element.15) | data formatting | bytes 4128768 | tf_op jit(solution)/shard_map/add | solution.py:53
  19.0 2.3 %sub.231 = f32[144,3584]{1,0:T(8,128)S(1)} reshape(f32[16,9,3584]{2,1,0:T(8,128)} %get-tuple-element.14) | data formatting | bytes 4128768 | tf_op jit(solution)/shard_map/sub | solution.py:50
  21.3 0.1 fusion.29
  21.4 0.3 fusion.13
  21.8 47.2 %all-gather.2.cloned.1.call-done = bf16[512,7168]{1,0:T(8,128)(2,1)} async-done(((bf16[32,7168]{1,0:T(8,128)(2,1)}), bf16[512,7168]{1,0:T(8,128)(2,1)}) %all-gather.2.cloned.1.call-update) | async-done | bytes 7340048 | tf_op jit(solution)/shard_map/all_gather | solution.py:104
  69.0 10.2 %convert_element_type.131 = f32[512,7168]{1,0:T(8,128)} convert(bf16[512,7168]{1,0:T(8,128)(2,1)} %all-gather.2.cloned.1.call-done) | non-fusion elementwise | flops 3670016 | bytes 22020096 | tf_op jit(solution)/shard_map/convert_element_type | solution.py:108
  79.3 6.1 %fusion.2 = f32[512]{0:T(512)S(1)} fusion(f32[512,7168]{1,0:T(8,128)} %convert_element_type.131, f32[3584]{0:T(1024)S(1)} %copy-done.5), kind=kLoop, calls=%fused_computation.3 | loop fusion | flops 9174528 | bytes 14696448 | tf_op jit(solution)/shard_map/reduce_sum | solution.py:109
  85.3 1.2 copy-done.1
  86.6 0.6 copy-done.3
  87.2 1.3 fusion.3
  88.5 1.5 %fusion.16 = (f32[144]{0:T(256)S(1)}, f32[144,512]{1,0:T(8,128)S(1)}) fusion(f32[144]{0:T(256)S(1)} %add_multiply_fusion.2, f32[512]{0:T(512)S(1)} %add.205, f32[512]{0:T(512)S(1)} %fusion.2, f32[144,512]{1,0:T(8,128)S(1)} %fusion.3, bf16[512,7168]{1,0:T(8,128)(2,1)S(1)} %copy-done.1, f32[144,3584]{1,0:T(8,128)S(1)} %sub.231, ...), kind=kOutput, calls=%fused_computation.34 | convolution fusion | flops 529883008 | bytes 6346304 | tf_op jit(solution)/shard_map/dot_general | solution.py:70
  90.0 0.1 reduce_max.14
  90.1 0.1 reduce_max.18
  90.2 0.1 sub.253
  90.3 0.1 sub.254
  90.4 0.2 exponential_reduce_fusion
  90.6 0.1 reduce_sum.45
  90.7 0.1 reduce_sum.46
  90.9 0.1 sub.260
  91.0 0.1 subtract_exponential_fusion
  91.2 1.0 fusion.34
  92.2 0.1 copy.19
  92.4 0.5 convolution_bitcast_fusion
  92.9 0.7 multiply_reduce_fusion.3
  93.7 0.1 concatenate.9
  93.8 0.1 concatenate.8
  94.0 0.9 fusion.12
  94.8 5.0 %all-to-all-start = ((f32[16,8,448]{2,1,0:T(8,128)}), f32[16,8,448]{2,1,0:T(8,128)S(1)}, u32[]{:S(2)}, u32[]{:S(2)}) async-start(f32[16,8,448]{2,1,0:T(8,128)} %fusion.12), calls=%async_computation | async-start | bytes 524288 | tf_op jit(solution)/shard_map/all_to_all | solution.py:17
  99.8 0.1 add_multiply_fusion.1
  99.9 7.5 %all-to-all-done = f32[16,8,448]{2,1,0:T(8,128)S(1)} async-done(((f32[16,8,448]{2,1,0:T(8,128)}), f32[16,8,448]{2,1,0:T(8,128)S(1)}, u32[]{:S(2)}, u32[]{:S(2)}) %all-to-all-start) | async-done | bytes 229408 | tf_op jit(solution)/shard_map/all_to_all | solution.py:17
  107.5 0.1 reshape.307
  107.7 0.7 copy.22
  108.4 15.0 %all-to-all-start.1 = ((f32[32,8,14]{2,1,0:T(8,128)}), f32[32,8,14]{2,1,0:T(8,128)S(1)}, u32[]{:S(2)}, u32[]{:S(2)}) async-start(f32[32,8,14]{2,1,0:T(8,128)} %copy.22), calls=%async_computation.1 | async-start | bytes 262144 | tf_op jit(solution)/shard_map/all_to_all | solution.py:17
  123.3 0.1 add_subtract_fusion
  123.5 0.9 copy.23
  124.4 15.4 %all-to-all-done.1 = f32[32,8,14]{2,1,0:T(8,128)S(1)} async-done(((f32[32,8,14]{2,1,0:T(8,128)}), f32[32,8,14]{2,1,0:T(8,128)S(1)}, u32[]{:S(2)}, u32[]{:S(2)}) %all-to-all-start.1) | async-done | bytes 14368 | tf_op jit(solution)/shard_map/all_to_all | solution.py:17
  139.8 0.6 reduce_sum.48
  (32 shorter events, 0.4 us)
Async XLA Ops:
  7.2 14.1 %copy-start = (f32[8]{0:T(128)S(1)}, f32[8]{0:T(128)}, u32[]{:S(2)}) copy-start(f32[8]{0:T(128)} %param.14) | copy-start | bytes 100
  7.2 61.9 %all-gather.2.cloned.1.call-start = ((), (), s32[]{:S(2)}) async-start(), calls=%async_computation.2 | async-start | bytes 7798784 | tf_op jit(solution)/shard_map/all_gather | solution.py:104
  19.0 2.3 %copy-start.6 = (s32[512]{0:T(512)S(1)}, s32[512]{0:T(512)}, u32[]{:S(2)}) copy-start(s32[512]{0:T(512)} %param.12) | copy-start | bytes 6148
  19.0 2.5 %copy-start.7 = (s32[512]{0:T(512)S(1)}, s32[512]{0:T(512)}, u32[]{:S(2)}) copy-start(s32[512]{0:T(512)} %param.13) | copy-start | bytes 6148
  19.0 2.5 %copy-start.8 = (f32[64]{0:T(128)S(1)}, f32[64]{0:T(128)}, u32[]{:S(2)}) copy-start(f32[64]{0:T(128)} %param.15) | copy-start | bytes 772
  19.0 2.8 %copy-start.5 = (f32[3584]{0:T(1024)S(1)}, f32[3584]{0:T(1024)}, u32[]{:S(2)}) copy-start(f32[3584]{0:T(1024)} %param.11) | copy-start | bytes 43012
  79.3 7.3 %copy-start.1 = (bf16[512,7168]{1,0:T(8,128)(2,1)S(1)}, bf16[512,7168]{1,0:T(8,128)(2,1)}, u32[]{:S(2)}) copy-start(bf16[512,7168]{1,0:T(8,128)(2,1)} %all-gather.2.cloned.1.call-done) | copy-start | bytes 22020100
  79.3 7.9 %copy-start.3 = (f32[144,3584]{1,0:T(8,128)S(1)}, f32[144,3584]{1,0:T(8,128)}, u32[]{:S(2)}) copy-start(f32[144,3584]{1,0:T(8,128)} %add.202) | copy-start | bytes 6193156
  88.5 3.9 %copy-start.2 = (bf16[16,7168]{1,0:T(8,128)(2,1)S(1)}, bf16[16,7168]{1,0:T(8,128)(2,1)}, u32[]{:S(2)}) copy-start(bf16[16,7168]{1,0:T(8,128)(2,1)} %param.8) | copy-start | bytes 688132
  90.0 2.9 %copy-start.4 = (f32[3584,9]{0,1:T(8,128)S(1)}, f32[3584,9]{0,1:T(8,128)}, u32[]{:S(2)}) copy-start(f32[3584,9]{0,1:T(8,128)} %get-tuple-element.19) | copy-start | bytes 387076
  94.8 12.6 %all-to-all-start = ((f32[16,8,448]{2,1,0:T(8,128)}), f32[16,8,448]{2,1,0:T(8,128)S(1)}, u32[]{:S(2)}, u32[]{:S(2)}) async-start(f32[16,8,448]{2,1,0:T(8,128)} %fusion.12), calls=%async_computation | async-start | bytes 524288 | tf_op jit(solution)/shard_map/all_to_all | solution.py:17
  108.4 31.5 %all-to-all-start.1 = ((f32[32,8,14]{2,1,0:T(8,128)}), f32[32,8,14]{2,1,0:T(8,128)S(1)}, u32[]{:S(2)}, u32[]{:S(2)}) async-start(f32[32,8,14]{2,1,0:T(8,128)} %copy.22), calls=%async_computation.1 | async-start | bytes 262144 | tf_op jit(solution)/shard_map/all_to_all | solution.py:17
Sparse Core Ops, SparseCore 0:
  10.1 58.8 all-gather.1
where the time goes:
time: 148 us; the launch traced here: 147 us
  waiting for transfers between devices  70.9 us (48%)
  other arithmetic  25 us (17%)
  starting transfers between devices  20 us (14%)
  between operations  14.3 us (10%)
  local copies, waits for them, and re-layouts  11.5 us (8%)
  matrix products  5.57 us (4%)
    all_gather x1, waiting for transfers between devices, local(): segment = lax.all_gather(references, 'ref', axis=0, tiled=True)  47.2 us
    all_to_all x2, waiting for transfers between devices, sum_at_owner(): lax.all_to_all(in_blocks(shard, dim, length), axis, 0, 0, tiled=True)  23 us
    all_to_all x2, starting transfers between devices, sum_at_owner(): lax.all_to_all(in_blocks(shard, dim, length), axis, 0, 0, tiled=True)  19.9 us
    convert_element_type x1, other arithmetic, local(): wide = segment.astype(jnp.float32)  10.2 us
    reduce_sum x1, other arithmetic, local(): jnp.sum(noise_weight[None, :] * (wide[:, :coef_total] * wide[:, :coef_tot...  6.08 us
    sub x1, other arithmetic, aligned_stack(): real_part[:, None, :] * cosine_table[None]  4 us
    add x1, local copies, waits for them, and re-layouts, aligned_stack(): real_part[:, None, :] * sine_table[None]  3.22 us
  transfers between devices with their start and end apart: 3, of which 3 were waited for; matrix products, arithmetic and copies ran while one was open for 10% of the time, Pallas kernels for 0%

commit v1 on v0

--- a/solution.py
+++ b/solution.py
@@ -101,7 +101,9 @@
     prior = jnp.dot(class_table, class_logprior, precision=lax.Precision.HIGHEST) + jnp.dot(
         orient_table, orient_logprior, precision=lax.Precision.HIGHEST
     )
-    segment = lax.all_gather(references, "ref", axis=0, tiled=True)
+    segment = jnp.concatenate(
+        lax.all_to_all(jnp.stack([references] * lax.axis_size("ref")), "ref", 0, 0), axis=0
+    )
     cross_piece = contract(scaled_real, segment[:, :coef_total]) + contract(
         scaled_imag, segment[:, coef_total:]
     )

time: 148 us -> 204 us (1.38)
  waiting for transfers between devices: 70.9 us -> 125 us
  between operations: 14.3 us -> 0.94 us
  starting transfers between devices: 20 us -> 30.1 us
  matrix products: 5.57 us -> 9.68 us
  local copies, waits for them, and re-layouts: 11.5 us -> 13.7 us
    all_to_all x0 -> x1, waiting for transfers between devices: none -> 102 us  [local(): lax.all_to_all(jnp.stack([references] * lax.axis_size('ref')), 'ref', 0, 0)]
    all_gather x1 -> x0, waiting for transfers between devices: 47.2 us -> none  [local(): segment = lax.all_gather(references, 'ref', axis=0, tiled=True)]
    all_to_all x0 -> x1, starting transfers between devices: none -> 5.59 us  [local(): lax.all_to_all(jnp.stack([references] * lax.axis_size('ref')), 'ref', 0, 0)]
    another operation x0 -> x1, local copies, waits for them, and re-layouts: none -> 4.9 us  [local(): jnp.stack([references] * lax.axis_size('ref'))]
    all_to_all x2, starting transfers between devices: 19.9 us -> 24.5 us  [sum_at_owner(): lax.all_to_all(in_blocks(shard, dim, length), axis, 0, 0, tiled=True)]
    dot_general x2, matrix products: 2.82 us -> 6.93 us  [contract(): lax.dot_general(left, right, (((1,), (1,)), ((), ())), preferred_element_...]
  transfers between devices with their start and end apart: 3 -> 3, of which waited for: 3 -> 3; matrix products, arithmetic and copies ran while one was open for 10% -> 7% of each run, Pallas kernels for 0% -> 0%
where the time goes in v1:
time: 204 us
  waiting for transfers between devices  125 us (61%)
  starting transfers between devices  30.1 us (15%)
  other arithmetic  24.4 us (12%)
  local copies, waits for them, and re-layouts  13.7 us (7%)
  matrix products  9.68 us (5%)
    all_to_all x1, waiting for transfers between devices, local(): lax.all_to_all(jnp.stack([references] * lax.axis_size('ref')), 'ref', 0, 0)  102 us
    all_to_all x2, starting transfers between devices, sum_at_owner(): lax.all_to_all(in_blocks(shard, dim, length), axis, 0, 0, tiled=True)  24.5 us
    all_to_all x2, waiting for transfers between devices, sum_at_owner(): lax.all_to_all(in_blocks(shard, dim, length), axis, 0, 0, tiled=True)  23 us
    convert_element_type x1, other arithmetic, local(): wide = segment.astype(jnp.float32)  10.2 us
    dot_general x2, matrix products, contract(): lax.dot_general(left, right, (((1,), (1,)), ((), ())), preferred_element_...  6.93 us
    reduce_sum x1, other arithmetic, local(): jnp.sum(noise_weight[None, :] * (wide[:, :coef_total] * wide[:, :coef_tot...  6.08 us
    all_to_all x1, starting transfers between devices, local(): lax.all_to_all(jnp.stack([references] * lax.axis_size('ref')), 'ref', 0, 0)  5.59 us
    another operation x1, local copies, waits for them, and re-layouts, local(): jnp.stack([references] * lax.axis_size('ref'))  4.9 us
  transfers between devices with their start and end apart: 3, of which 3 were waited for; matrix products, arithmetic and copies ran while one was open for 7% of the time, Pallas kernels for 0%

profile of v1, /device:TPU:32, one launch (start us, length us, event | category | flops | bytes accessed | tf_op | source)
XLA Modules:
  0.0 203.9 jit_solution(12452139134189205153)
XLA Ops:
  0.6 0.0 copy-start
  0.6 4.9 %stack.2 = bf16[16,32,7168]{2,1,0:T(8,128)(2,1)} broadcast(bf16[32,7168]{1,0:T(8,128)(2,1)} %param.10), dimensions={1,2} | broadcast | bytes 7798784 | tf_op jit(solution)/shard_map/stack | solution.py:105
  5.5 5.6 %all-to-all-start = ((bf16[16,32,7168]{2,1,0:T(8,128)(2,1)}), bf16[16,32,7168]{2,1,0:T(8,128)(2,1)}, u32[]{:S(2)}, u32[]{:S(2)}) async-start(bf16[16,32,7168]{2,1,0:T(8,128)(2,1)} %stack.2), calls=%async_computation | async-start | bytes 14680064 | tf_op jit(solution)/shard_map/all_to_all | solution.py:105
  11.2 0.1 sub.250
  11.3 0.1 sub.241
  11.4 0.1 sub.251
  11.5 0.1 sub.246
  11.6 0.1 sub.236
  11.6 0.1 sub.247
  11.8 1.6 fusion.23
  13.4 4.1 %multiply_subtract_fusion = (f32[16,9,3584]{2,1,0:T(8,128)}, f32[16,9,3584]{2,1,0:T(8,128)}) fusion(f32[9,3584]{1,0:T(8,128)S(1)} %get-tuple-element.20, f32[16,3584]{1,0:T(8,128)S(1)} %get-tuple-element.17, f32[9,3584]{1,0:T(8,128)S(1)} %get-tuple-element.21, f32[16,3584]{1,0:T(8,128)S(1)} %get-tuple-element.16), kind=kLoop, calls=%fused_computation.12 | loop fusion | flops 3096576 | bytes 4845568 | tf_op jit(solution)/shard_map/sub | solution.py:50
  17.5 3.2 %add.202 = f32[144,3584]{1,0:T(8,128)} reshape(f32[16,9,3584]{2,1,0:T(8,128)} %get-tuple-element.15) | data formatting | bytes 4128768 | tf_op jit(solution)/shard_map/add | solution.py:53
  20.7 2.3 %sub.231 = f32[144,3584]{1,0:T(8,128)S(1)} reshape(f32[16,9,3584]{2,1,0:T(8,128)} %get-tuple-element.14) | data formatting | bytes 4128768 | tf_op jit(solution)/shard_map/sub | solution.py:50
  23.0 0.1 fusion.29
  23.2 0.3 fusion.13
  23.5 102.1 %all-to-all-done = bf16[16,32,7168]{2,1,0:T(8,128)(2,1)} async-done(((bf16[16,32,7168]{2,1,0:T(8,128)(2,1)}), bf16[16,32,7168]{2,1,0:T(8,128)(2,1)}, u32[]{:S(2)}, u32[]{:S(2)}) %all-to-all-start) | async-done | bytes 7340064 | tf_op jit(solution)/shard_map/all_to_all | solution.py:105
  125.6 10.2 %convert_element_type.131 = f32[512,7168]{1,0:T(8,128)} convert(bf16[512,7168]{1,0:T(8,128)(2,1)} %bitcast.8) | non-fusion elementwise | flops 3670016 | bytes 22020096 | tf_op jit(solution)/shard_map/convert_element_type | solution.py:110
  135.8 6.1 %fusion.2 = f32[512]{0:T(512)S(1)} fusion(f32[512,7168]{1,0:T(8,128)} %convert_element_type.131, f32[3584]{0:T(1024)S(1)} %copy-done.4), kind=kLoop, calls=%fused_computation.3 | loop fusion | flops 9174528 | bytes 14696448 | tf_op jit(solution)/shard_map/reduce_sum | solution.py:111
  141.9 3.4 %fusion.3 = f32[144,512]{1,0:T(8,128)S(1)} fusion(bf16[512,7168]{1,0:T(8,128)(2,1)} %bitcast.8, f32[144,3584]{1,0:T(8,128)S(1)} %copy-done.2, f32[3584]{0:T(1024)S(1)} %broadcast_multiply_fusion), kind=kOutput, calls=%fused_computation.7 | convolution fusion | flops 529514496 | bytes 6043648 | tf_op jit(solution)/shard_map/dot_general | solution.py:70
  145.3 3.5 %fusion.16 = (f32[144]{0:T(256)S(1)}, f32[144,512]{1,0:T(8,128)S(1)}) fusion(f32[144]{0:T(256)S(1)} %add_multiply_fusion.2, f32[512]{0:T(512)S(1)} %add.205, f32[512]{0:T(512)S(1)} %fusion.2, f32[144,512]{1,0:T(8,128)S(1)} %fusion.3, bf16[512,7168]{1,0:T(8,128)(2,1)} %bitcast.8, f32[144,3584]{1,0:T(8,128)S(1)} %sub.231, f32[3584]{0:T(1024)S(1)} %broadcast_multiply_fusion), kind=kOutput, calls=%fused_computation.34 | convolution fusion | flops 529883008 | bytes 6343808 | tf_op jit(solution)/shard_map/dot_general | solution.py:70
  148.9 0.0 copy-start.3
  148.9 0.1 reduce_max.14
  149.0 0.1 reduce_max.18
  149.1 0.1 sub.253
  149.1 0.1 sub.254
  149.2 0.2 exponential_reduce_fusion
  149.5 0.1 reduce_sum.45
  149.6 0.1 reduce_sum.46
  149.7 0.1 sub.259
  149.8 0.1 sub.260
  149.9 0.1 subtract_exponential_fusion
  150.1 1.0 fusion.34
  151.1 0.1 copy.19
  151.2 0.5 convolution_bitcast_fusion
  151.8 0.7 multiply_reduce_fusion.3
  152.6 0.1 concatenate.9
  152.7 0.1 concatenate.8
  152.8 0.9 fusion.12
  153.7 6.8 %all-to-all-start.1 = ((f32[16,8,448]{2,1,0:T(8,128)}), f32[16,8,448]{2,1,0:T(8,128)S(1)}, u32[]{:S(2)}, u32[]{:S(2)}) async-start(f32[16,8,448]{2,1,0:T(8,128)} %fusion.12), calls=%async_computation.1 | async-start | bytes 524288 | tf_op jit(solution)/shard_map/all_to_all | solution.py:17
  160.5 0.1 add_multiply_fusion.1
  160.6 7.5 %all-to-all-done.1 = f32[16,8,448]{2,1,0:T(8,128)S(1)} async-done(((f32[16,8,448]{2,1,0:T(8,128)}), f32[16,8,448]{2,1,0:T(8,128)S(1)}, u32[]{:S(2)}, u32[]{:S(2)}) %all-to-all-start.1) | async-done | bytes 229408 | tf_op jit(solution)/shard_map/all_to_all | solution.py:17
  168.2 0.1 reshape.313
  168.3 0.7 copy.22
  169.1 17.7 %all-to-all-start.2 = ((f32[32,8,14]{2,1,0:T(8,128)}), f32[32,8,14]{2,1,0:T(8,128)S(1)}, u32[]{:S(2)}, u32[]{:S(2)}) async-start(f32[32,8,14]{2,1,0:T(8,128)} %copy.22), calls=%async_computation.2 | async-start | bytes 262144 | tf_op jit(solution)/shard_map/all_to_all | solution.py:17
  186.8 0.1 add_subtract_fusion
  186.9 0.9 copy.23
  187.8 15.4 %all-to-all-done.2 = f32[32,8,14]{2,1,0:T(8,128)S(1)} async-done(((f32[32,8,14]{2,1,0:T(8,128)}), f32[32,8,14]{2,1,0:T(8,128)S(1)}, u32[]{:S(2)}, u32[]{:S(2)}) %all-to-all-start.2) | async-done | bytes 14368 | tf_op jit(solution)/shard_map/all_to_all | solution.py:17
  203.2 0.6 reduce_sum.48
  (32 shorter events, 0.3 us)
Async XLA Ops:
  0.6 22.4 %copy-start = (f32[8]{0:T(128)S(1)}, f32[8]{0:T(128)}, u32[]{:S(2)}) copy-start(f32[8]{0:T(128)} %param.14) | copy-start | bytes 100
  5.5 5.7 %copy-start.7 = (s32[16]{0:T(128)S(1)}, s32[16]{0:T(128)}, u32[]{:S(2)}) copy-start(s32[16]{0:T(128)} %param.9) | copy-start | bytes 196
  5.5 6.2 %copy-start.1 = (bf16[16,7168]{1,0:T(8,128)(2,1)S(1)}, bf16[16,7168]{1,0:T(8,128)(2,1)}, u32[]{:S(2)}) copy-start(bf16[16,7168]{1,0:T(8,128)(2,1)} %param.8) | copy-start | bytes 688132
  5.5 120.1 %all-to-all-start = ((bf16[16,32,7168]{2,1,0:T(8,128)(2,1)}), bf16[16,32,7168]{2,1,0:T(8,128)(2,1)}, u32[]{:S(2)}, u32[]{:S(2)}) async-start(bf16[16,32,7168]{2,1,0:T(8,128)(2,1)} %stack.2), calls=%async_computation | async-start | bytes 14680064 | tf_op jit(solution)/shard_map/all_to_all | solution.py:105
  20.7 2.3 %copy-start.5 = (s32[512]{0:T(512)S(1)}, s32[512]{0:T(512)}, u32[]{:S(2)}) copy-start(s32[512]{0:T(512)} %param.12) | copy-start | bytes 6148
  20.7 2.5 %copy-start.6 = (s32[512]{0:T(512)S(1)}, s32[512]{0:T(512)}, u32[]{:S(2)}) copy-start(s32[512]{0:T(512)} %param.13) | copy-start | bytes 6148
  20.7 2.5 %copy-start.8 = (f32[64]{0:T(128)S(1)}, f32[64]{0:T(128)}, u32[]{:S(2)}) copy-start(f32[64]{0:T(128)} %param.15) | copy-start | bytes 772
  20.7 2.8 %copy-start.4 = (f32[3584]{0:T(1024)S(1)}, f32[3584]{0:T(1024)}, u32[]{:S(2)}) copy-start(f32[3584]{0:T(1024)} %param.11) | copy-start | bytes 43012
  135.8 6.1 %copy-start.2 = (f32[144,3584]{1,0:T(8,128)S(1)}, f32[144,3584]{1,0:T(8,128)}, u32[]{:S(2)}) copy-start(f32[144,3584]{1,0:T(8,128)} %add.202) | copy-start | bytes 6193156
  148.9 2.9 %copy-start.3 = (f32[3584,9]{0,1:T(8,128)S(1)}, f32[3584,9]{0,1:T(8,128)}, u32[]{:S(2)}) copy-start(f32[3584,9]{0,1:T(8,128)} %get-tuple-element.19) | copy-start | bytes 387076
  153.7 14.5 %all-to-all-start.1 = ((f32[16,8,448]{2,1,0:T(8,128)}), f32[16,8,448]{2,1,0:T(8,128)S(1)}, u32[]{:S(2)}, u32[]{:S(2)}) async-start(f32[16,8,448]{2,1,0:T(8,128)} %fusion.12), calls=%async_computation.1 | async-start | bytes 524288 | tf_op jit(solution)/shard_map/all_to_all | solution.py:17
  169.1 34.2 %all-to-all-start.2 = ((f32[32,8,14]{2,1,0:T(8,128)}), f32[32,8,14]{2,1,0:T(8,128)S(1)}, u32[]{:S(2)}, u32[]{:S(2)}) async-start(f32[32,8,14]{2,1,0:T(8,128)} %copy.22), calls=%async_computation.2 | async-start | bytes 262144 | tf_op jit(solution)/shard_map/all_to_all | solution.py:17
